TPU v7x, 32 devices: a whole 2x2x4 slice. The times are simulated.
32 devices in a mesh: dp: 4 (over z), seq: 4 (over x, core), tensor: 2 (over y).
Axes of the slice: x: 2, y: 2, z: 4, core: 2. Of those that a mesh axis runs over, the one named last changes fastest.
Arguments:
- latent_embed: bfloat16 [20480, 2, 1024], P(('dp', 'seq'), None, 'tensor'), may hold values from -6 to 6
- adapter: bfloat16 [2, 1024, 1024], P(None, 'tensor'), may hold values from -0.125 to 0.125
- first_gain: float32 [1024], replicated, may hold values from 0.5 to 1.5
- query_weight: bfloat16 [1024, 1024], P(None, 'tensor'), may hold values from -0.1875 to 0.1875
- key_weight: bfloat16 [1024, 1024], P(None, 'tensor'), may hold values from -0.1875 to 0.1875
- value_weight: bfloat16 [1024, 1024], P(None, 'tensor'), may hold values from -0.1875 to 0.1875
- output_weight: bfloat16 [1024, 1024], P('tensor'), may hold values from -0.1875 to 0.1875
- second_gain: float32 [1024], replicated, may hold values from 0.5 to 1.5
- third_gain: float32 [1024], replicated, may hold values from 0.5 to 1.5
- gate_weight: bfloat16 [1024, 2816], P(None, 'tensor'), may hold values from -0.1875 to 0.1875
- up_weight: bfloat16 [1024, 2816], P(None, 'tensor'), may hold values from -0.1875 to 0.1875
- down_weight: bfloat16 [2816, 1024], P('tensor'), may hold values from -0.109375 to 0.109375
- fourth_gain: float32 [1024], replicated, may hold values from 0.5 to 1.5
- parents: int32 [4, 20], P('dp'), may hold values from -1 to 19, as said below
- positions: int32 [20480], P(('dp', 'seq')), may hold values from 0 to 2559, as said below
- cotangent: bfloat16 [20480, 1024], P(('dp', 'seq')), may hold values from -6 to 6
Outputs:
- layer_out: float32 [20480, 1024], P(('dp', 'seq'))
- latent_gradient: float32 [20480, 2, 1024], P(('dp', 'seq'), None, 'tensor')
- adapter_gradient: float32 [2, 1024, 1024], P(None, 'tensor')
- first_gain_gradient: float32 [1024], replicated
- query_gradient: float32 [1024, 1024], P(None, 'tensor')
- key_gradient: float32 [1024, 1024], P(None, 'tensor')
- value_gradient: float32 [1024, 1024], P(None, 'tensor')
- output_gradient: float32 [1024, 1024], P('tensor')
- second_gain_gradient: float32 [1024], replicated
- third_gain_gradient: float32 [1024], replicated
- gate_gradient: float32 [1024, 2816], P(None, 'tensor')
- up_gradient: float32 [1024, 2816], P(None, 'tensor')
- down_gradient: float32 [2816, 1024], P('tensor')
- fourth_gain_gradient: float32 [1024], replicated
Inputs may be any that keep to these rules, and one draw needn't show every extreme that they name: `parents`: each tree's segments form a trunk of 8 chained segments from the root, 4 branches whose parent is the trunk's last segment and 2 leaves under each branch; which segment number plays which role is drawn. `positions`: a token's position is 256 times the number of its segment's ancestors plus its place inside its segment.
All inputs are finite; a program needn't handle non-finite values.
Results may differ from a plain program's by a relative error of at most 0.025.
Values may be sent and summed in bfloat16 or wider, within the bound.
A program may use at most 896 MiB of HBM per device.

v0:
```python
import jax
import jax.numpy as jnp
from jax import lax
from jax.sharding import PartitionSpec as P

DH = 64
SEG = 256
EPSILON = 1e-06
THETA = 50000.0


def normalize(values, gain):
    scale = lax.rsqrt(jnp.mean(values * values, axis=-1, keepdims=True) + EPSILON)
    normed = values * scale
    return (normed * gain, normed, scale)


def normalize_back(upstream, gain, normed, scale):
    scaled = upstream * gain
    inward = scale * (scaled - normed * jnp.mean(scaled * normed, axis=-1, keepdims=True))
    return (inward, jnp.sum(upstream * normed, axis=0))


def angles(positions, width):
    half = width // 2
    freq = THETA ** (-jnp.arange(half, dtype=jnp.float32) * 2.0 / width)
    angle = positions.astype(jnp.float32)[:, None] * freq[None, :]
    return (jnp.cos(angle)[:, None, :], jnp.sin(angle)[:, None, :])


def rotate(values, cosine, sine, sign):
    half = values.shape[-1] // 2
    first = values[..., :half]
    second = values[..., half:]
    return jnp.concatenate(
        [first * cosine - sign * second * sine, second * cosine + sign * first * sine], axis=-1
    )


def ancestry(parent_row):
    labels = jnp.arange(parent_row.shape[0], dtype=jnp.int32)

    def extend(index, state):
        current, total = state
        total = total | (current[:, None] == labels[None, :])
        current = jnp.where(current >= 0, jnp.take(parent_row, jnp.maximum(current, 0)), -1)
        return (current, total)

    start = (parent_row, jnp.zeros((parent_row.shape[0], parent_row.shape[0]), jnp.bool_))
    current, total = lax.fori_loop(0, parent_row.shape[0], extend, start)
    return total


def path_mask(parent_row, query_ids, key_ids):
    table = ancestry(parent_row)
    query_seg = query_ids // SEG
    key_seg = key_ids // SEG
    far = jnp.take(jnp.take(table, query_seg, axis=0), key_seg, axis=1)
    near = (query_seg[:, None] == key_seg[None, :]) & (key_ids[None, :] <= query_ids[:, None])
    return far | near


def on_device(
    latent_embed,
    adapter,
    first_gain,
    query_weight,
    key_weight,
    value_weight,
    output_weight,
    second_gain,
    third_gain,
    gate_weight,
    up_weight,
    down_weight,
    fourth_gain,
    parents,
    positions,
    cotangent,
):
    rows = latent_embed.shape[0]
    local_heads = query_weight.shape[1] // DH
    scale = DH ** (-0.5)
    adapted = lax.psum(
        jnp.einsum("rcd,cde->re", latent_embed, adapter, preferred_element_type=jnp.float32),
        "tensor",
    )
    first_out, first_normed, first_scale = normalize(adapted, first_gain)
    first_low = first_out.astype(jnp.bfloat16)
    cosine, sine = angles(positions, DH)
    query_raw = jnp.dot(first_low, query_weight, preferred_element_type=jnp.float32).reshape(
        rows, local_heads, DH
    )
    queries = rotate(query_raw, cosine, sine, 1.0).astype(jnp.bfloat16)
    key_raw = jnp.dot(first_low, key_weight, preferred_element_type=jnp.float32).reshape(
        rows, local_heads, DH
    )
    keys_local = rotate(key_raw, cosine, sine, 1.0).astype(jnp.bfloat16)
    values_local = (
        jnp.dot(first_low, value_weight, preferred_element_type=jnp.float32)
        .astype(jnp.bfloat16)
        .reshape(rows, local_heads, DH)
    )
    keys_all, values_all = (
        lax.all_gather(keys_local, "seq", axis=0, tiled=True),
        lax.all_gather(values_local, "seq", axis=0, tiled=True),
    )
    tree_rows = keys_all.shape[0]
    query_ids = lax.axis_index("seq") * rows + jnp.arange(rows, dtype=jnp.int32)
    key_ids = jnp.arange(tree_rows, dtype=jnp.int32)
    allowed = path_mask(parents[0], query_ids, key_ids)[None]

    def score_block(keys):
        raw = jnp.einsum("qhd,khd->hqk", queries, keys, preferred_element_type=jnp.float32) * scale
        return jnp.where(allowed, raw, -1e30)

    scores = score_block(keys_all)
    top = jnp.max(scores, axis=-1, keepdims=True)
    weights = jnp.exp(scores - top)
    total = jnp.sum(weights, axis=-1, keepdims=True)
    probs = weights / total
    logsum = top + jnp.log(total)
    attended = jnp.einsum(
        "hqk,khd->qhd", probs.astype(jnp.bfloat16), values_all, preferred_element_type=jnp.float32
    )
    attended = attended.reshape(rows, local_heads * DH).astype(jnp.bfloat16)
    attention = lax.psum(
        jnp.dot(attended, output_weight, preferred_element_type=jnp.float32).astype(jnp.bfloat16),
        "tensor",
    ).astype(jnp.float32)
    second_out, second_normed, second_scale = normalize(attention, second_gain)
    middle = adapted + second_out
    third_out, third_normed, third_scale = normalize(middle, third_gain)
    third_low = third_out.astype(jnp.bfloat16)
    gate = jnp.dot(third_low, gate_weight, preferred_element_type=jnp.float32)
    upward = jnp.dot(third_low, up_weight, preferred_element_type=jnp.float32)
    hidden = (jax.nn.silu(gate) * upward).astype(jnp.bfloat16)
    mixed = lax.psum(
        jnp.dot(hidden, down_weight, preferred_element_type=jnp.float32).astype(jnp.bfloat16),
        "tensor",
    ).astype(jnp.float32)
    fourth_out, fourth_normed, fourth_scale = normalize(mixed, fourth_gain)
    layer_out = middle + fourth_out
    upstream = cotangent.astype(jnp.float32)
    mixed_back, fourth_gain_part = normalize_back(
        upstream, fourth_gain, fourth_normed, fourth_scale
    )
    mixed_low = mixed_back.astype(jnp.bfloat16)
    down_part = jnp.einsum("rf,rd->fd", hidden, mixed_low, preferred_element_type=jnp.float32)
    hidden_back = (
        jnp.einsum("rd,fd->rf", mixed_low, down_weight, preferred_element_type=jnp.float32)
        .astype(jnp.bfloat16)
        .astype(jnp.float32)
    )
    swiglu_value, product_back = jax.vjp(
        lambda left, right: jax.nn.silu(left) * right, gate, upward
    )
    gate_back, up_back = product_back(hidden_back)
    gate_low = gate_back.astype(jnp.bfloat16)
    up_low = up_back.astype(jnp.bfloat16)
    gate_part = jnp.einsum("rd,rf->df", third_low, gate_low, preferred_element_type=jnp.float32)
    up_part = jnp.einsum("rd,rf->df", third_low, up_low, preferred_element_type=jnp.float32)
    third_term = jnp.einsum(
        "rf,df->rd", gate_low, gate_weight, preferred_element_type=jnp.float32
    ) + jnp.einsum("rf,df->rd", up_low, up_weight, preferred_element_type=jnp.float32)
    third_back = lax.psum(third_term.astype(jnp.bfloat16), "tensor").astype(jnp.float32)
    middle_part, third_gain_part = normalize_back(third_back, third_gain, third_normed, third_scale)
    middle_back = upstream + middle_part
    attention_back, second_gain_part = normalize_back(
        middle_back, second_gain, second_normed, second_scale
    )
    attention_low = attention_back.astype(jnp.bfloat16)
    output_part = jnp.einsum(
        "re,rd->ed", attended, attention_low, preferred_element_type=jnp.float32
    )
    attended_back = (
        jnp.einsum("rd,ed->re", attention_low, output_weight, preferred_element_type=jnp.float32)
        .astype(jnp.bfloat16)
        .reshape(rows, local_heads, DH)
    )
    keys_back, values_back = (
        lax.all_gather(keys_local, "seq", axis=0, tiled=True),
        lax.all_gather(values_local, "seq", axis=0, tiled=True),
    )
    probs_back = jnp.exp(score_block(keys_back) - logsum)
    prob_grad = jnp.einsum(
        "qhd,khd->hqk", attended_back, values_back, preferred_element_type=jnp.float32
    )
    score_grad = (
        probs_back * (prob_grad - jnp.sum(prob_grad * probs_back, axis=-1, keepdims=True))
    ).astype(jnp.bfloat16)
    query_rot = (
        jnp.einsum("hqk,khd->qhd", score_grad, keys_back, preferred_element_type=jnp.float32)
        * scale
    )
    key_rot_all = (
        jnp.einsum("hqk,qhd->khd", score_grad, queries, preferred_element_type=jnp.float32) * scale
    )
    value_back_all = jnp.einsum(
        "hqk,qhd->khd",
        probs_back.astype(jnp.bfloat16),
        attended_back,
        preferred_element_type=jnp.float32,
    )
    key_rot, value_back = (
        lax.psum_scatter(
            key_rot_all.astype(jnp.bfloat16), "seq", scatter_dimension=0, tiled=True
        ).astype(jnp.float32),
        lax.psum_scatter(
            value_back_all.astype(jnp.bfloat16), "seq", scatter_dimension=0, tiled=True
        ).astype(jnp.float32),
    )
    query_low = (
        rotate(query_rot, cosine, sine, -1.0).astype(jnp.bfloat16).reshape(rows, local_heads * DH)
    )
    key_low = (
        rotate(key_rot, cosine, sine, -1.0).astype(jnp.bfloat16).reshape(rows, local_heads * DH)
    )
    value_low = value_back.astype(jnp.bfloat16).reshape(rows, local_heads * DH)
    query_part = jnp.einsum("rd,re->de", first_low, query_low, preferred_element_type=jnp.float32)
    key_part = jnp.einsum("rd,re->de", first_low, key_low, preferred_element_type=jnp.float32)
    value_part = jnp.einsum("rd,re->de", first_low, value_low, preferred_element_type=jnp.float32)
    first_term = jnp.einsum(
        "re,de->rd", query_low, query_weight, preferred_element_type=jnp.float32
    )
    first_term = first_term + jnp.einsum(
        "re,de->rd", key_low, key_weight, preferred_element_type=jnp.float32
    )
    first_term = first_term + jnp.einsum(
        "re,de->rd", value_low, value_weight, preferred_element_type=jnp.float32
    )
    first_back = lax.psum(first_term.astype(jnp.bfloat16), "tensor").astype(jnp.float32)
    adapted_part, first_gain_part = normalize_back(
        first_back, first_gain, first_normed, first_scale
    )
    adapted_low = (middle_back + adapted_part).astype(jnp.bfloat16)
    latent_gradient = jnp.einsum(
        "re,cde->rcd", adapted_low, adapter, preferred_element_type=jnp.float32
    )
    adapter_part = jnp.einsum(
        "rcd,re->cde", latent_embed, adapted_low, preferred_element_type=jnp.float32
    )
    summed = (
        lax.psum(gate_part.astype(jnp.bfloat16), ("dp", "seq")).astype(jnp.float32),
        lax.psum(up_part.astype(jnp.bfloat16), ("dp", "seq")).astype(jnp.float32),
        lax.psum(down_part.astype(jnp.bfloat16), ("dp", "seq")).astype(jnp.float32),
        lax.psum(third_gain_part.astype(jnp.bfloat16), ("dp", "seq")).astype(jnp.float32),
        lax.psum(fourth_gain_part.astype(jnp.bfloat16), ("dp", "seq")).astype(jnp.float32),
        lax.psum(query_part.astype(jnp.bfloat16), ("dp", "seq")).astype(jnp.float32),
        lax.psum(key_part.astype(jnp.bfloat16), ("dp", "seq")).astype(jnp.float32),
        lax.psum(value_part.astype(jnp.bfloat16), ("dp", "seq")).astype(jnp.float32),
        lax.psum(output_part.astype(jnp.bfloat16), ("dp", "seq")).astype(jnp.float32),
        lax.psum(first_gain_part.astype(jnp.bfloat16), ("dp", "seq")).astype(jnp.float32),
        lax.psum(second_gain_part.astype(jnp.bfloat16), ("dp", "seq")).astype(jnp.float32),
        lax.psum(adapter_part.astype(jnp.bfloat16), ("dp", "seq")).astype(jnp.float32),
    )
    gate_total, up_total, down_total, third_total, fourth_total = (
        summed[0],
        summed[1],
        summed[2],
        summed[3],
        summed[4],
    )
    query_total, key_total, value_total, output_total, first_total, second_total = (
        summed[5],
        summed[6],
        summed[7],
        summed[8],
        summed[9],
        summed[10],
    )
    adapter_total = summed[11]
    return (
        layer_out,
        latent_gradient,
        adapter_total,
        first_total,
        query_total,
        key_total,
        value_total,
        output_total,
        second_total,
        third_total,
        gate_total,
        up_total,
        down_total,
        fourth_total,
    )


def solution(mesh):
    in_specs = (
        P(("dp", "seq"), None, "tensor"),
        P(None, "tensor", None),
        P(),
        P(None, "tensor"),
        P(None, "tensor"),
        P(None, "tensor"),
        P("tensor", None),
        P(),
        P(),
        P(None, "tensor"),
        P(None, "tensor"),
        P("tensor", None),
        P(),
        P("dp", None),
        P(("dp", "seq")),
        P(("dp", "seq"), None),
    )
    out_specs = (
        P(("dp", "seq"), None),
        P(("dp", "seq"), None, "tensor"),
        P(None, "tensor", None),
        P(),
        P(None, "tensor"),
        P(None, "tensor"),
        P(None, "tensor"),
        P("tensor", None),
        P(),
        P(),
        P(None, "tensor"),
        P(None, "tensor"),
        P("tensor", None),
        P(),
    )
    return jax.shard_map(
        on_device, mesh=mesh, in_specs=in_specs, out_specs=out_specs, check_vma=False
    )
```

profile of v0, /device:TPU:0, one launch (start us, length us, event | category | flops | bytes accessed | tf_op | source)
XLA Modules:
  0.0 1609.6 jit_solution(6540593411886035098)
XLA Ops:
  7.2 7.8 convolution_bitcast_fusion
  17.1 131.4 %all-reduce.9.cloned.1.call-done = f32[1280,1024]{1,0:T(8,128)} async-done(((f32[1280,1024]{1,0:T(8,128)}), f32[1280,1024]{1,0:T(8,128)}) %all-reduce.9.cloned.1.call-update) | async-done | bytes 5242896 | tf_op jit(solution)/shard_map/psum | solution.py:84
  148.4 3.0 multiply_reduce_fusion.2
  153.7 1.7 fusion.78
  155.7 1.6 fusion.77
  157.4 1.8 subtract_convert_fusion.3
  160.6 16.5 %while.13 = (s32[]{:T(128)}, s32[20]{0:T(128)S(1)}, pred[20,20]{1,0:T(8,128)(4,1)S(1)}, s32[20]{0:T(128)S(1)}, s32[]{:T(128)}, /*index=5*/s32[]{:T(128)}) while((s32[]{:T(128)}, s32[20]{0:T(128)S(1)}, pred[20,20]{1,0:T(8,128)(4,1)S(1)}, s32[20]{0:T(128)S(1)}, s32[]{:T(128)}, /*index=5*/s32[]{:T(128)}) %tuple.77), condition=%wide.region_3.0_spmd.clone, body=%wide.region_2.3_spmd.clone.sunk | while | flops 2347 | bytes 5775 | solution.py:50
  177.1 2.6 gather_fusion.1
  180.3 22.2 %gather_fusion.2 = pred[5120,1280]{1,0:T(8,128)(4,1)} fusion(pred[1280,20]{0,1:T(8,128)(4,1)S(1)} %copy.38, s32[5120]{0:T(1024)S(1)} %broadcast_clamp_fusion), kind=kCustom, calls=%fused_computation.2 | custom fusion | bytes 13127680 | tf_op jit(solution)/shard_map/jit(_take)/gather | solution.py:58
  202.5 11.1 fusion.10
  213.6 16.6 %copy.39 = pred[1280,5120]{1,0:T(8,128)(4,1)} copy(pred[1280,5120]{0,1:T(8,128)(4,1)} %fusion.10) | data formatting | bytes 13107200 | tf_op jit(solution)/shard_map/or | solution.py:60
  230.2 4.7 convolution_convert_fusion.7
  235.0 74.7 %fusion.76 = (f32[8,1280]{1,0:T(8,128)}, f32[8,1280,5120]{2,1,0:T(8,128)}) fusion(bf16[5120,8,64]{0,2,1:T(8,128)(2,1)} %all-gather.5.cloned.1.call-done, bf16[1280,8,32]{0,2,1:T(8,128)(2,1)} %get-tuple-element.126, bf16[1280,8,32]{0,2,1:T(8,128)(2,1)S(1)} %copy-done.20, pred[1280,5120]{1,0:T(8,128)(4,1)} %copy.39), kind=kOutput, calls=%fused_computation.170 | convolution fusion | flops 6870784000 | bytes 222863360 | tf_op jit(solution)/shard_map/qhd,khd->hqk/dot_general | solution.py:114
  309.7 63.5 %fusion.3 = f32[8,1280]{1,0:T(8,128)S(1)} fusion(f32[8,1280,5120]{2,1,0:T(8,128)} %get-tuple-element.137, f32[8,1280]{1,0:T(8,128)} %get-tuple-element.136), kind=kLoop, calls=%fused_computation.16 | loop fusion | flops 104847360 | bytes 209797120 | tf_op jit(solution)/shard_map/reduce_sum | solution.py:120
  373.2 68.2 %fusion.56 = bf16[8,64,1280]{2,1,0:T(8,128)(2,1)} fusion(bf16[5120,8,64]{0,2,1:T(8,128)(2,1)} %all-gather.3.cloned.1.call-done, f32[8,1280,5120]{2,1,0:T(8,128)} %get-tuple-element.137, f32[8,1280]{1,0:T(8,128)S(1)} %fusion.3, f32[8,1280]{1,0:T(8,128)S(1)} %copy-done.43), kind=kOutput, calls=%fused_computation.97 | convolution fusion | flops 6868828160 | bytes 216350720 | tf_op jit(solution)/shard_map/hqk,khd->qhd/dot_general | solution.py:123
  441.4 4.7 convolution_convert_fusion.1
  446.4 74.6 %all-reduce.11.cloned.1.call-done = bf16[1280,1024]{1,0:T(8,128)(2,1)} async-done(((bf16[1280,1024]{1,0:T(8,128)(2,1)}), bf16[1280,1024]{1,0:T(8,128)(2,1)}) %all-reduce.11.cloned.1.call-update) | async-done | bytes 2621456 | tf_op jit(solution)/shard_map/psum | solution.py:127
  521.0 2.5 fusion.48
  523.5 3.9 multiply_reduce_fusion.1
  527.9 2.1 copy-done.6
  531.1 4.3 fusion.79
  535.4 6.6 multiply_convert_fusion.2
  542.1 1.8 copy-done.69
  543.9 5.5 convolution_convert_fusion.5
  549.9 74.0 %all-reduce.13.cloned.1.call-done = bf16[1280,1024]{1,0:T(8,128)(2,1)} async-done(((bf16[1280,1024]{1,0:T(8,128)(2,1)}), bf16[1280,1024]{1,0:T(8,128)(2,1)}) %all-reduce.13.cloned.1.call-update) | async-done | bytes 2621456 | tf_op jit(solution)/shard_map/psum | solution.py:138
  623.9 2.5 fusion.51
  626.5 4.3 fusion.54
  630.7 11.4 fusion.14
  642.1 4.3 fusion.80
  646.4 5.7 add_convert_fusion.1
  652.3 8.8 convolution_convert_fusion.3
  661.1 6.0 convolution_convert_fusion.2
  667.1 59.6 %all-reduce.15.cloned.1.call-done = bf16[1280,1024]{1,0:T(8,128)(2,1)} async-done(((bf16[1280,1024]{1,0:T(8,128)(2,1)}), bf16[1280,1024]{1,0:T(8,128)(2,1)}) %all-reduce.15.cloned.1.call-update) | async-done | bytes 2621456 | tf_op jit(solution)/shard_map/psum | solution.py:166
  726.7 5.6 fusion.52
  732.3 8.5 fusion.47
  744.7 138.2 %multiply_reduce_fusion = (f32[8,1280]{1,0:T(8,128)S(1)}, f32[8,1280,5120]{2,1,0:T(8,128)}) fusion(f32[8,1280,5120]{2,1,0:T(8,128)} %get-tuple-element.137, f32[8,1280]{1,0:T(8,128)S(1)} %log_add_fusion, bf16[1280,8,64]{0,2,1:T(8,128)(2,1)S(1)} %bitcast.82, bf16[5120,8,64]{0,2,1:T(8,128)(2,1)} %all-gather.3.cloned.1.call-done), kind=kOutput, calls=%fused_computation.11 | convolution fusion | flops 6868162560 | bytes 426065920 | tf_op jit(solution)/shard_map/qhd,khd->hqk/dot_general | solution.py:186
  882.9 160.8 %multiply_convert_fusion = bf16[8,1280,5120]{2,1,0:T(8,128)(2,1)} fusion(f32[8,1280,5120]{2,1,0:T(8,128)} %get-tuple-element.141, f32[8,1280,5120]{2,1,0:T(8,128)} %get-tuple-element.137, f32[8,1280]{1,0:T(8,128)S(1)} %get-tuple-element.140, f32[8,1280]{1,0:T(8,128)S(1)} %log_add_fusion), kind=kLoop, calls=%fused_computation.10 | loop fusion | flops 209715200 | bytes 524369920 | tf_op jit(solution)/shard_map/convert_element_type | solution.py:191
  1043.7 37.6 %fusion.55 = bf16[5120,8,64]{0,2,1:T(8,128)(2,1)} fusion(bf16[8,1280,5120]{2,1,0:T(8,128)(2,1)} %multiply_convert_fusion, bf16[1280,8,32]{0,2,1:T(8,128)(2,1)S(1)} %copy-done.22, bf16[1280,8,32]{0,2,1:T(8,128)(2,1)S(1)} %copy-done.21), kind=kOutput, calls=%fused_computation.82 | convolution fusion | flops 6718750720 | bytes 111411200 | tf_op jit(solution)/shard_map/hqk,qhd->khd/dot_general | solution.py:197
  1082.6 71.0 %fusion.19 = bf16[5120,8,64]{0,2,1:T(8,128)(2,1)} fusion(bf16[1280,8,64]{0,2,1:T(8,128)(2,1)S(1)} %bitcast.83, f32[8,1280,5120]{2,1,0:T(8,128)} %get-tuple-element.137, f32[8,1280]{1,0:T(8,128)S(1)} %log_add_fusion), kind=kOutput, calls=%fused_computation.40 | convolution fusion | flops 6818365440 | bytes 216309760 | tf_op jit(solution)/shard_map/hqk,qhd->khd/dot_general | solution.py:199
  1153.6 44.4 %multiply_bitcast_fusion = f32[1280,8,64]{0,2,1:T(8,128)S(1)} fusion(bf16[5120,8,64]{0,2,1:T(8,128)(2,1)} %all-gather.5.cloned.1.call-done, bf16[8,1280,5120]{2,1,0:T(8,128)(2,1)} %multiply_convert_fusion), kind=kOutput, calls=%fused_computation.99 | convolution fusion | flops 6711541760 | bytes 112721920 | tf_op jit(solution)/shard_map/hqk,khd->qhd/dot_general | solution.py:193
  1198.0 1.6 convert_element_type.215
  1202.1 3.9 fusion.81
  1206.1 3.9 fusion.82
  1210.0 7.9 add_convert_fusion
  1218.0 8.0 convolution_convert_fusion.4
  1226.1 2.5 convolution_convert_fusion.8
  1228.6 2.6 convolution_convert_fusion.9
  1231.1 2.6 convolution_convert_fusion.10
  1233.7 2.6 convolution_convert_fusion.11
  1236.3 56.2 %all-reduce.17.cloned.1.call-done = bf16[1280,1024]{1,0:T(8,128)(2,1)} async-done(((bf16[1280,1024]{1,0:T(8,128)(2,1)}), bf16[1280,1024]{1,0:T(8,128)(2,1)}) %all-reduce.17.cloned.1.call-update) | async-done | bytes 2621456 | tf_op jit(solution)/shard_map/psum | solution.py:232
  1292.5 5.0 fusion.53
  1297.5 5.0 fusion.57
  1304.0 4.1 convert_bitcast_fusion
  1308.8 36.3 %all-reduce = (bf16[1024]{0:T(1024)(128)(2,1)S(1)}, bf16[1024]{0:T(1024)(128)(2,1)S(1)}, bf16[1024]{0:T(1024)(128)(2,1)S(1)}, bf16[1024]{0:T(1024)(128)(2,1)S(1)}) all-reduce(bf16[1024]{0:T(1024)(128)(2,1)S(1)} %get-tuple-element.91, bf16[1024]{0:T(1024)(128)(2,1)S(1)} %copy-done.52, ...), channel_id=1, replica_groups=mesh['dp'=4,'seq'=4,'tensor'=2] {'dp','seq'}, use_global_device_ids=true, to_apply=%region_22.23 | all-reduce | flops 4096 | bytes 16384 | tf_op jit(solution)/shard_map/psum | solution.py:253
  1347.5 4.6 fusion.83
  1352.1 10.7 copy.42
  1362.8 219.9 %all-reduce.19.cloned.1.call-done = (bf16[2,512,1024]{1,2,0:T(8,128)(2,1)}, bf16[1024,512]{1,0:T(8,128)(2,1)}, bf16[1024,512]{1,0:T(8,128)(2,1)}, bf16[1024,512]...) async-done(((bf16[2,512,1024]{1,2,0:T(8,128)(2,1)}, ...) | async-done | bytes 14942224 | tf_op jit(solution)/shard_map/psum | solution.py:255
  1582.6 4.2 copy.43
  1586.8 1.6 convert_element_type.229
  1588.4 1.6 convert_element_type.231
  1590.1 1.6 convert_element_type.233
  1593.3 2.9 convert_element_type.241
  1596.3 2.9 convert_element_type.243
  1599.2 3.2 convert_element_type.245
  (301 shorter events, 39.4 us)
Async XLA Ops:
  7.2 536.7 %copy-start = (bf16[1408,1024]{1,0:T(8,128)(2,1)S(1)}, bf16[1408,1024]{1,0:T(8,128)(2,1)}, u32[]{:S(2)}) copy-start(bf16[1408,1024]{1,0:T(8,128)(2,1)} %param.29) | copy-start | bytes 8650756
  7.2 141.2 %all-reduce.9.cloned.1.call-start = ((), (), s32[]{:S(2)}) async-start(), calls=%async_computation.2 | async-start | bytes 10485760 | tf_op jit(solution)/shard_map/psum | solution.py:84
  15.0 136.5 %copy-start.48 = (f32[1024]{0:T(1024)S(1)}, f32[1024]{0:T(1024)}, u32[]{:S(2)}) copy-start(f32[1024]{0:T(1024)} %param.20) | copy-start | bytes 12292
  15.1 219.9 %all-gather.5.cloned.1.call-start = ((), (), s32[]{:S(2)}) async-start(), calls=%async_computation.4 | async-start | bytes 6553600 | tf_op jit(solution)/shard_map/all_gather | solution.py:105
  17.1 140.3 %copy-start.31 = (f32[1280,32]{0,1:T(8,128)}, f32[1280,32]{0,1:T(8,128)S(1)}, u32[]{:S(2)}) copy-start(f32[1280,32]{0,1:T(8,128)S(1)} %get-tuple-element.135) | copy-start | bytes 491524
  148.4 4.0 copy-start.5
  160.4 212.8 %all-gather.3.cloned.1.call-start = ((), (), s32[]{:S(2)}) async-start(), calls=%async_computation.3 | async-start | bytes 6553600 | tf_op jit(solution)/shard_map/all_gather | solution.py:106
  230.2 4.8 copy-start.20
  234.9 286.1 %all-reduce.11.cloned.1.call-start = ((), (), s32[]{:S(2)}) async-start(), calls=%async_computation.5 | async-start | bytes 5242880 | tf_op jit(solution)/shard_map/psum | solution.py:127
  309.7 63.5 %copy-start.43 = (f32[8,1280]{1,0:T(8,128)S(1)}, f32[8,1280]{1,0:T(8,128)}, u32[]{:S(2)}) copy-start(f32[8,1280]{1,0:T(8,128)} %get-tuple-element.136) | copy-start | bytes 122884
  446.1 77.4 %copy-start.47 = (f32[1024]{0:T(1024)S(1)}, f32[1024]{0:T(1024)}, u32[]{:S(2)}) copy-start(f32[1024]{0:T(1024)} %param.25) | copy-start | bytes 12292
  446.1 177.8 %all-reduce.13.cloned.1.call-start = ((), (), s32[]{:S(2)}) async-start(), calls=%async_computation.6 | async-start | bytes 5242880 | tf_op jit(solution)/shard_map/psum | solution.py:138
  521.0 2.5 copy-start.8
  523.5 3.9 copy-start.46
  527.4 2.7 copy-start.6
  527.4 3.7 copy-start.55
  531.1 4.3 copy-start.27
  531.1 4.3 copy-start.57
  535.4 6.6 copy-start.68
  549.4 77.0 %copy-start.50 = (f32[1024]{0:T(1024)S(1)}, f32[1024]{0:T(1024)}, u32[]{:S(2)}) copy-start(f32[1024]{0:T(1024)} %param.30) | copy-start | bytes 12292
  549.4 177.2 %all-reduce.15.cloned.1.call-start = ((), (), s32[]{:S(2)}) async-start(), calls=%async_computation.7 | async-start | bytes 5242880 | tf_op jit(solution)/shard_map/psum | solution.py:166
  623.9 2.5 copy-start.10
  623.9 6.8 copy-start.15
  630.7 11.4 copy-start.56
  642.1 4.3 copy-start.66
  642.1 4.3 copy-start.58
  642.1 4.3 copy-start.67
  652.2 545.9 %reduce-scatter.3.cloned.1.call-start = ((), (), s32[]{:S(2)}) async-start(), calls=%async_computation.8 | async-start | bytes 6553600 | tf_op jit(solution)/shard_map/reduce_scatter | solution.py:206
  652.2 8.9 copy-start.11
  652.2 8.9 copy-start.16
  652.3 8.9 copy-start.70
  667.1 65.2 %copy-start.9 = (bf16[1280,1024]{1,0:T(8,128)(2,1)S(1)}, bf16[1280,1024]{1,0:T(8,128)(2,1)}, u32[]{:S(2)}) copy-start(bf16[1280,1024]{1,0:T(8,128)(2,1)} %all-reduce.11.cloned.1.call-done) | copy-start | bytes 7864324
  726.7 5.6 copy-start.12
  726.7 5.6 copy-start.13
  740.7 2.4 copy-start.7
  740.7 2.4 copy-start.60
  744.7 138.2 %copy-start.3 = (bf16[1280,512]{0,1:T(8,128)(2,1)}, bf16[1280,512]{0,1:T(8,128)(2,1)S(1)}, u32[]{:S(2)}) copy-start(bf16[1280,512]{0,1:T(8,128)(2,1)S(1)} %convolution_convert_fusion.6) | copy-start | bytes 3932164
  882.9 160.8 %copy-start.21 = (bf16[1280,8,32]{0,2,1:T(8,128)(2,1)S(1)}, bf16[1280,8,32]{0,2,1:T(8,128)(2,1)}, u32[]{:S(2)}) copy-start(bf16[1280,8,32]{0,2,1:T(8,128)(2,1)} %get-tuple-element.125) | copy-start | bytes 1966084
  882.9 160.8 %copy-start.22 = (bf16[1280,8,32]{0,2,1:T(8,128)(2,1)S(1)}, bf16[1280,8,32]{0,2,1:T(8,128)(2,1)}, u32[]{:S(2)}) copy-start(bf16[1280,8,32]{0,2,1:T(8,128)(2,1)} %get-tuple-element.126) | copy-start | bytes 1966084
  1081.3 128.7 %reduce-scatter.5.cloned.1.call-start = ((), (), s32[]{:S(2)}) async-start(), calls=%async_computation.9 | async-start | bytes 6553600 | tf_op jit(solution)/shard_map/reduce_scatter | solution.py:209
  1153.6 138.9 %all-reduce.17.cloned.1.call-start = ((), (), s32[]{:S(2)}) async-start(), calls=%async_computation.10 | async-start | bytes 5242880 | tf_op jit(solution)/shard_map/psum | solution.py:232
  1200.5 5.5 copy-start.33
  1200.6 5.4 copy-start.35
  1202.1 3.9 copy-start.64
  1210.0 8.0 copy-start.28
  1218.0 364.7 %all-reduce.19.cloned.1.call-start = ((), (), s32[]{:S(2)}) async-start(), calls=%async_computation.11 | async-start | bytes 29884416 | tf_op jit(solution)/shard_map/psum | solution.py:255
  1218.0 8.0 copy-start.30
  1218.0 8.0 copy-start.65
  1226.0 2.5 copy-start.26
  1226.1 2.5 copy-start.37
  1228.6 2.6 copy-start.34
  1231.1 2.6 copy-start.36
  1233.7 58.8 %copy-start.45 = (f32[1280]{0:T(1024)S(1)}, f32[1280]{0:T(1024)}, u32[]{:S(2)}) copy-start(f32[1280]{0:T(1024)} %copy-done.44) | copy-start | bytes 15364
  1233.7 58.8 %copy-start.49 = (f32[1024]{0:T(1024)S(1)}, f32[1024]{0:T(1024)}, u32[]{:S(2)}) copy-start(f32[1024]{0:T(1024)} %param.20) | copy-start | bytes 12292
  1292.5 5.0 copy-start.14
  1297.5 6.5 copy-start.59
  1308.1 39.4 %copy-start.24 = (bf16[1280,1024,1]{1,0,2:T(8,128)(2,1)S(1)}, bf16[1280,1024,1]{1,0,2:T(8,128)(2,1)}, u32[]{:S(2)}) copy-start(bf16[1280,1024,1]{1,0,2:T(8,128)(2,1)} %copy-done.23) | copy-start | bytes 7864324
  1582.6 4.2 copy-start.41
  1586.8 3.2 copy-start.39
  1588.4 3.2 copy-start.38
  1590.1 3.2 copy-start.19
  1593.2 3.0 copy-start.18
  1596.2 3.0 copy-start.17
  1599.2 3.3 copy-start.1
  (17 other events, 21.9 us)
Sparse Core Ops, SparseCore 0:
  15.2 133.2 all-reduce.8
  160.5 40.4 all-gather.4
  235.0 40.4 all-gather.2
  446.3 74.7 all-reduce.10
  549.6 74.3 all-reduce.12
  652.3 74.3 all-reduce.14
  1081.4 51.3 reduce-scatter.2
  1153.7 51.3 reduce-scatter.4
  1218.1 74.3 all-reduce.16
  1308.2 274.3 all-reduce.18
where the time goes:
time: 1620 us; the launch traced here: 1610 us
  waiting for transfers between devices  616 us (38%)
  matrix products  551 us (34%)
  other arithmetic  305 us (19%)
  local copies, waits for them, and re-layouts  84.2 us (5%)
  blocking collectives  36.3 us (2%)
    psum x1, waiting for transfers between devices, on_device(): lax.psum(adapter_part.astype(jnp.bfloat16), ('dp', 'seq'))  220 us
    convert_element_type x1, other arithmetic, on_device(): score_grad = (probs_back * (prob_grad - jnp.sum(prob_grad * probs_back, a...  161 us
    dot_general x1, matrix products, on_device(): jnp.einsum('qhd,khd->hqk', attended_back, values_back, preferred_element_...  138 us
    psum x1, waiting for transfers between devices, on_device(): lax.psum(jnp.einsum('rcd,cde->re', latent_embed, adapter, preferred_eleme...  131 us
    dot_general x1, matrix products, score_block(): jnp.einsum('qhd,khd->hqk', queries, keys, preferred_element_type=jnp.floa...  74.7 us
    psum x1, waiting for transfers between devices, on_device(): lax.psum(jnp.dot(attended, output_weight, preferred_element_type=jnp.floa...  74.6 us
    psum x1, waiting for transfers between devices, on_device(): lax.psum(jnp.dot(hidden, down_weight, preferred_element_type=jnp.float32)...  74 us
    dot_general x1, matrix products, on_device(): jnp.einsum('hqk,qhd->khd', probs_back.astype(jnp.bfloat16), attended_back...  71 us
  transfers between devices with their start and end apart: 10, of which 6 were waited for; matrix products, arithmetic and copies ran while one was open for 24% of the time, Pallas kernels for 0%

commit v1 on v0

--- a/solution.py
+++ b/solution.py
@@ -7,6 +7,11 @@
 SEG = 256
 EPSILON = 1e-06
 THETA = 50000.0
+
+
+def one_after_other(value, one, other):
+    partial = lax.psum(value, one)
+    return lax.psum(partial, other)
 
 
 def normalize(values, gain):
@@ -252,7 +257,7 @@
         lax.psum(output_part.astype(jnp.bfloat16), ("dp", "seq")).astype(jnp.float32),
         lax.psum(first_gain_part.astype(jnp.bfloat16), ("dp", "seq")).astype(jnp.float32),
         lax.psum(second_gain_part.astype(jnp.bfloat16), ("dp", "seq")).astype(jnp.float32),
-        lax.psum(adapter_part.astype(jnp.bfloat16), ("dp", "seq")).astype(jnp.float32),
+        one_after_other(adapter_part.astype(jnp.bfloat16), "seq", "dp").astype(jnp.float32),
     )
     gate_total, up_total, down_total, third_total, fourth_total = (
         summed[0],

time: 1620 us -> 1730 us (1.068)
  waiting for transfers between devices: 616 us -> 727 us
    psum x1 -> x3, waiting for transfers between devices: 220 us -> 299 us  [the longest x1 245 us: on_device(): lax.psum(query_part.astype(jnp.bfloat16), ('dp', 'seq')).astype(jnp.float32)]
    psum x1, waiting for transfers between devices: 56.2 us -> 74.2 us  [on_device(): lax.psum(first_term.astype(jnp.bfloat16), 'tensor').astype(jnp.float32)]
  transfers between devices with their start and end apart: 10 -> 12, of which waited for: 6 -> 8; matrix products, arithmetic and copies ran while one was open for 24% -> 23% of each run, Pallas kernels for 0% -> 0%
where the time goes in v1:
time: 1730 us; the launch traced here: 1720 us
  waiting for transfers between devices  727 us (42%)
  matrix products  551 us (32%)
  other arithmetic  307 us (18%)
  local copies, waits for them, and re-layouts  83.9 us (5%)
  blocking collectives  35.2 us (2%)
    psum x1, waiting for transfers between devices, on_device(): lax.psum(query_part.astype(jnp.bfloat16), ('dp', 'seq')).astype(jnp.float32)  245 us
    convert_element_type x1, other arithmetic, on_device(): score_grad = (probs_back * (prob_grad - jnp.sum(prob_grad * probs_back, a...  161 us
    dot_general x1, matrix products, on_device(): jnp.einsum('qhd,khd->hqk', attended_back, values_back, preferred_element_...  138 us
    psum x1, waiting for transfers between devices, on_device(): lax.psum(jnp.einsum('rcd,cde->re', latent_embed, adapter, preferred_eleme...  131 us
    dot_general x1, matrix products, score_block(): jnp.einsum('qhd,khd->hqk', queries, keys, preferred_element_type=jnp.floa...  74.7 us
    psum x1, waiting for transfers between devices, on_device(): lax.psum(jnp.dot(attended, output_weight, preferred_element_type=jnp.floa...  74.6 us
    psum x1, waiting for transfers between devices, on_device(): lax.psum(third_term.astype(jnp.bfloat16), 'tensor').astype(jnp.float32)  74.2 us
    psum x1, waiting for transfers between devices, on_device(): lax.psum(first_term.astype(jnp.bfloat16), 'tensor').astype(jnp.float32)  74.2 us
  transfers between devices with their start and end apart: 12, of which 8 were waited for; matrix products, arithmetic and copies ran while one was open for 23% of the time, Pallas kernels for 0%

profile of v1, /device:TPU:0, one launch (start us, length us, event | category | flops | bytes accessed | tf_op | source)
XLA Modules:
  0.0 1721.8 jit_solution(2626691891238002628)
XLA Ops:
  7.2 7.8 convolution_bitcast_fusion
  17.1 131.4 %all-reduce.11.cloned.1.call-done = f32[1280,1024]{1,0:T(8,128)} async-done(((f32[1280,1024]{1,0:T(8,128)}), f32[1280,1024]{1,0:T(8,128)}) %all-reduce.11.cloned.1.call-update) | async-done | bytes 5242896 | tf_op jit(solution)/shard_map/psum | solution.py:89
  148.4 3.0 multiply_reduce_fusion.2
  153.7 1.7 fusion.78
  155.7 1.7 fusion.77
  157.4 1.8 subtract_convert_fusion.3
  160.6 16.5 while.13
  177.1 2.6 gather_fusion.1
  180.3 22.2 %gather_fusion.2 = pred[5120,1280]{1,0:T(8,128)(4,1)} fusion(pred[1280,20]{0,1:T(8,128)(4,1)S(1)} %copy.38, s32[5120]{0:T(1024)S(1)} %broadcast_clamp_fusion), kind=kCustom, calls=%fused_computation.2 | custom fusion | bytes 13127680 | tf_op jit(solution)/shard_map/jit(_take)/gather | solution.py:63
  202.5 11.1 fusion.10
  213.6 16.5 copy.39
  230.2 4.7 convolution_convert_fusion.7
  235.0 74.7 %fusion.76 = (f32[8,1280]{1,0:T(8,128)}, f32[8,1280,5120]{2,1,0:T(8,128)}) fusion(bf16[5120,8,64]{0,2,1:T(8,128)(2,1)} %all-gather.5.cloned.1.call-done, bf16[1280,8,32]{0,2,1:T(8,128)(2,1)} %get-tuple-element.125, bf16[1280,8,32]{0,2,1:T(8,128)(2,1)S(1)} %copy-done.20, pred[1280,5120]{1,0:T(8,128)(4,1)} %copy.39), kind=kOutput, calls=%fused_computation.170 | convolution fusion | flops 6870784000 | bytes 222863360 | tf_op jit(solution)/shard_map/qhd,khd->hqk/dot_general | solution.py:119
  309.7 63.5 %fusion.3 = f32[8,1280]{1,0:T(8,128)S(1)} fusion(f32[8,1280,5120]{2,1,0:T(8,128)} %get-tuple-element.136, f32[8,1280]{1,0:T(8,128)} %get-tuple-element.135), kind=kLoop, calls=%fused_computation.16 | loop fusion | flops 104847360 | bytes 209797120 | tf_op jit(solution)/shard_map/reduce_sum | solution.py:125
  373.2 68.2 %fusion.56 = bf16[8,64,1280]{2,1,0:T(8,128)(2,1)} fusion(bf16[5120,8,64]{0,2,1:T(8,128)(2,1)} %all-gather.3.cloned.1.call-done, f32[8,1280,5120]{2,1,0:T(8,128)} %get-tuple-element.136, f32[8,1280]{1,0:T(8,128)S(1)} %fusion.3, f32[8,1280]{1,0:T(8,128)S(1)} %copy-done.42), kind=kOutput, calls=%fused_computation.97 | convolution fusion | flops 6868828160 | bytes 216350720 | tf_op jit(solution)/shard_map/hqk,khd->qhd/dot_general | solution.py:128
  441.4 4.7 convolution_convert_fusion.1
  446.3 74.6 %all-reduce.13.cloned.1.call-done = bf16[1280,1024]{1,0:T(8,128)(2,1)} async-done(((bf16[1280,1024]{1,0:T(8,128)(2,1)}), bf16[1280,1024]{1,0:T(8,128)(2,1)}) %all-reduce.13.cloned.1.call-update) | async-done | bytes 2621456 | tf_op jit(solution)/shard_map/psum | solution.py:132
  520.9 2.5 fusion.48
  523.4 3.9 multiply_reduce_fusion.1
  527.9 2.1 copy-done.6
  531.0 4.3 fusion.79
  535.3 6.6 multiply_convert_fusion.2
  542.0 1.8 copy-done.73
  543.8 5.5 convolution_convert_fusion.5
  549.8 74.0 %all-reduce.15.cloned.1.call-done = bf16[1280,1024]{1,0:T(8,128)(2,1)} async-done(((bf16[1280,1024]{1,0:T(8,128)(2,1)}), bf16[1280,1024]{1,0:T(8,128)(2,1)}) %all-reduce.15.cloned.1.call-update) | async-done | bytes 2621456 | tf_op jit(solution)/shard_map/psum | solution.py:143
  623.8 2.5 fusion.51
  626.4 4.3 fusion.54
  630.6 11.4 fusion.14
  642.0 4.3 fusion.80
  646.3 5.7 add_convert_fusion.1
  652.4 74.2 %all-reduce.17.cloned.1.call-done = bf16[1280,1024]{1,0:T(8,128)(2,1)} async-done(((bf16[1280,1024]{1,0:T(8,128)(2,1)}), bf16[1280,1024]{1,0:T(8,128)(2,1)}) %all-reduce.17.cloned.1.call-update) | async-done | bytes 2621456 | tf_op jit(solution)/shard_map/psum | solution.py:171
  726.6 5.6 fusion.52
  732.2 8.5 fusion.47
  744.6 138.2 %multiply_reduce_fusion = (f32[8,1280]{1,0:T(8,128)S(1)}, f32[8,1280,5120]{2,1,0:T(8,128)}) fusion(f32[8,1280,5120]{2,1,0:T(8,128)} %get-tuple-element.136, f32[8,1280]{1,0:T(8,128)S(1)} %log_add_fusion, bf16[1280,8,64]{0,2,1:T(8,128)(2,1)S(1)} %bitcast.82, bf16[5120,8,64]{0,2,1:T(8,128)(2,1)} %all-gather.3.cloned.1.call-done), kind=kOutput, calls=%fused_computation.11 | convolution fusion | flops 6868162560 | bytes 426065920 | tf_op jit(solution)/shard_map/qhd,khd->hqk/dot_general | solution.py:191
  882.9 160.8 %multiply_convert_fusion = bf16[8,1280,5120]{2,1,0:T(8,128)(2,1)} fusion(f32[8,1280,5120]{2,1,0:T(8,128)} %get-tuple-element.140, f32[8,1280,5120]{2,1,0:T(8,128)} %get-tuple-element.136, f32[8,1280]{1,0:T(8,128)S(1)} %get-tuple-element.139, f32[8,1280]{1,0:T(8,128)S(1)} %log_add_fusion), kind=kLoop, calls=%fused_computation.10 | loop fusion | flops 209715200 | bytes 524369920 | tf_op jit(solution)/shard_map/convert_element_type | solution.py:196
  1043.7 37.4 %fusion.55 = bf16[5120,8,64]{0,2,1:T(8,128)(2,1)} fusion(bf16[8,1280,5120]{2,1,0:T(8,128)(2,1)} %multiply_convert_fusion, bf16[1280,8,32]{0,2,1:T(8,128)(2,1)S(1)} %copy-done.22, bf16[1280,8,32]{0,2,1:T(8,128)(2,1)S(1)} %copy-done.21), kind=kOutput, calls=%fused_computation.82 | convolution fusion | flops 6718750720 | bytes 111411200 | tf_op jit(solution)/shard_map/hqk,qhd->khd/dot_general | solution.py:202
  1082.4 71.0 %fusion.19 = bf16[5120,8,64]{0,2,1:T(8,128)(2,1)} fusion(bf16[1280,8,64]{0,2,1:T(8,128)(2,1)S(1)} %bitcast.83, f32[8,1280,5120]{2,1,0:T(8,128)} %get-tuple-element.136, f32[8,1280]{1,0:T(8,128)S(1)} %log_add_fusion), kind=kOutput, calls=%fused_computation.40 | convolution fusion | flops 6818365440 | bytes 216309760 | tf_op jit(solution)/shard_map/hqk,qhd->khd/dot_general | solution.py:204
  1153.4 44.0 %multiply_bitcast_fusion = f32[1280,8,64]{0,2,1:T(8,128)S(1)} fusion(bf16[5120,8,64]{0,2,1:T(8,128)(2,1)} %all-gather.5.cloned.1.call-done, bf16[8,1280,5120]{2,1,0:T(8,128)(2,1)} %multiply_convert_fusion), kind=kOutput, calls=%fused_computation.99 | convolution fusion | flops 6711541760 | bytes 112721920 | tf_op jit(solution)/shard_map/hqk,khd->qhd/dot_general | solution.py:198
  1197.4 1.7 convert_element_type.215
  1201.6 3.9 fusion.81
  1205.5 3.9 fusion.82
  1209.5 7.5 add_convert_fusion
  1217.5 74.2 %all-reduce.19.cloned.1.call-done = bf16[1280,1024]{1,0:T(8,128)(2,1)} async-done(((bf16[1280,1024]{1,0:T(8,128)(2,1)}), bf16[1280,1024]{1,0:T(8,128)(2,1)}) %all-reduce.19.cloned.1.call-update) | async-done | bytes 2621456 | tf_op jit(solution)/shard_map/psum | solution.py:237
  1291.7 5.0 fusion.53
  1296.8 5.0 fusion.57
  1303.3 4.1 convert_bitcast_fusion
  1307.5 8.8 convolution_convert_fusion.3
  1316.3 5.7 convolution_convert_fusion.2
  1322.1 36.8 %all-reduce.21.cloned.1.call-done = bf16[2,512,1024]{1,2,0:T(8,128)(2,1)} async-done(((bf16[2,512,1024]{1,2,0:T(8,128)(2,1)}), bf16[2,512,1024]{1,2,0:T(8,128)(2,1)}) %all-reduce.21.cloned.1.call-update) | async-done | bytes 2097168 | tf_op jit(solution)/shard_map/psum | solution.py:13
  1359.2 8.8 convolution_convert_fusion.4
  1368.0 2.6 convolution_convert_fusion.8
  1370.6 2.6 convolution_convert_fusion.9
  1373.2 2.6 convolution_convert_fusion.10
  1375.7 2.6 convolution_convert_fusion.11
  1379.0 35.2 %all-reduce = (bf16[1024]{0:T(1024)(128)(2,1)S(1)}, bf16[1024]{0:T(1024)(128)(2,1)S(1)}, bf16[1024]{0:T(1024)(128)(2,1)S(1)}, bf16[1024]{0:T(1024)(128)(2,1)S(1)}) all-reduce(bf16[1024]{0:T(1024)(128)(2,1)S(1)} %get-tuple-element.91, bf16[1024]{0:T(1024)(128)(2,1)S(1)} %copy-done.54, ...), channel_id=1, replica_groups=mesh['dp'=4,'seq'=4,'tensor'=2] {'dp','seq'}, use_global_device_ids=true, to_apply=%region_23.24 | all-reduce | flops 4096 | bytes 16384 | tf_op jit(solution)/shard_map/psum | solution.py:258
  1416.6 4.5 fusion.83
  1421.2 10.7 copy.42
  1431.9 16.5 all-reduce.23.cloned.1.call-done
  1448.4 4.1 copy.43
  1452.5 245.2 %all-reduce.25.cloned.1.call-done = (bf16[1024,512]{1,0:T(8,128)(2,1)}, bf16[1024,512]{1,0:T(8,128)(2,1)}, bf16[1024,512]{1,0:T(8,128)(2,1)}, bf16[512,1024]{1,0...) async-done(((bf16[1024,512]{1,0:T(8,128)(2,1)}, bf16[1024,512]{1,0:T(8,128)(2,1)}, bf16[1024,512]{1,0:T(8,128)(2,1)}, ...) | async-done | bytes 12845072 | tf_op jit(solution)/shard_map/psum | solution.py:254
  1697.7 3.0 convert_element_type.229
  1705.4 2.9 convert_element_type.241
  1708.4 2.9 convert_element_type.243
  1711.4 3.2 convert_element_type.245
  (315 shorter events, 43.5 us)
Async XLA Ops:
  7.2 536.6 %copy-start = (bf16[1408,1024]{1,0:T(8,128)(2,1)S(1)}, bf16[1408,1024]{1,0:T(8,128)(2,1)}, u32[]{:S(2)}) copy-start(bf16[1408,1024]{1,0:T(8,128)(2,1)} %param.29) | copy-start | bytes 8650756
  7.2 141.2 %all-reduce.11.cloned.1.call-start = ((), (), s32[]{:S(2)}) async-start(), calls=%async_computation.2 | async-start | bytes 10485760 | tf_op jit(solution)/shard_map/psum | solution.py:89
  15.0 136.5 %copy-start.49 = (f32[1024]{0:T(1024)S(1)}, f32[1024]{0:T(1024)}, u32[]{:S(2)}) copy-start(f32[1024]{0:T(1024)} %param.20) | copy-start | bytes 12292
  15.1 219.9 %all-gather.5.cloned.1.call-start = ((), (), s32[]{:S(2)}) async-start(), calls=%async_computation.4 | async-start | bytes 6553600 | tf_op jit(solution)/shard_map/all_gather | solution.py:110
  17.1 140.3 %copy-start.30 = (f32[1280,32]{0,1:T(8,128)}, f32[1280,32]{0,1:T(8,128)S(1)}, u32[]{:S(2)}) copy-start(f32[1280,32]{0,1:T(8,128)S(1)} %get-tuple-element.134) | copy-start | bytes 491524
  148.4 4.0 copy-start.5
  160.4 212.8 %all-gather.3.cloned.1.call-start = ((), (), s32[]{:S(2)}) async-start(), calls=%async_computation.3 | async-start | bytes 6553600 | tf_op jit(solution)/shard_map/all_gather | solution.py:111
  230.2 4.8 copy-start.20
  234.9 286.0 %all-reduce.13.cloned.1.call-start = ((), (), s32[]{:S(2)}) async-start(), calls=%async_computation.5 | async-start | bytes 5242880 | tf_op jit(solution)/shard_map/psum | solution.py:132
  309.7 63.5 %copy-start.42 = (f32[8,1280]{1,0:T(8,128)S(1)}, f32[8,1280]{1,0:T(8,128)}, u32[]{:S(2)}) copy-start(f32[8,1280]{1,0:T(8,128)} %get-tuple-element.135) | copy-start | bytes 122884
  446.0 77.4 %copy-start.48 = (f32[1024]{0:T(1024)S(1)}, f32[1024]{0:T(1024)}, u32[]{:S(2)}) copy-start(f32[1024]{0:T(1024)} %param.25) | copy-start | bytes 12292
  446.1 177.8 %all-reduce.15.cloned.1.call-start = ((), (), s32[]{:S(2)}) async-start(), calls=%async_computation.6 | async-start | bytes 5242880 | tf_op jit(solution)/shard_map/psum | solution.py:143
  523.4 3.9 copy-start.47
  527.3 2.7 copy-start.6
  527.3 3.7 copy-start.59
  531.0 4.3 copy-start.27
  531.0 4.3 copy-start.61
  535.3 6.6 copy-start.72
  549.3 77.0 %copy-start.51 = (f32[1024]{0:T(1024)S(1)}, f32[1024]{0:T(1024)}, u32[]{:S(2)}) copy-start(f32[1024]{0:T(1024)} %param.30) | copy-start | bytes 12292
  549.3 177.3 %all-reduce.17.cloned.1.call-start = ((), (), s32[]{:S(2)}) async-start(), calls=%async_computation.7 | async-start | bytes 5242880 | tf_op jit(solution)/shard_map/psum | solution.py:171
  623.8 6.8 copy-start.15
  626.4 105.8 %copy-start.45 = (f32[1280]{0:T(1024)}, f32[1280]{0:T(1024)S(1)}, u32[]{:S(2)}) copy-start(f32[1280]{0:T(1024)S(1)} %add_rsqrt_fusion) | copy-start | bytes 15364
  630.6 11.4 copy-start.56
  630.6 11.4 copy-start.60
  642.0 4.3 copy-start.70
  642.0 4.3 copy-start.62
  642.0 4.3 copy-start.71
  652.1 545.3 %reduce-scatter.3.cloned.1.call-start = ((), (), s32[]{:S(2)}) async-start(), calls=%async_computation.8 | async-start | bytes 6553600 | tf_op jit(solution)/shard_map/reduce_scatter | solution.py:211
  652.3 79.8 %copy-start.9 = (bf16[1280,1024]{1,0:T(8,128)(2,1)S(1)}, bf16[1280,1024]{1,0:T(8,128)(2,1)}, u32[]{:S(2)}) copy-start(bf16[1280,1024]{1,0:T(8,128)(2,1)} %all-reduce.13.cloned.1.call-done) | copy-start | bytes 7864324
  726.6 5.6 copy-start.11
  726.6 5.6 copy-start.13
  744.6 138.3 %copy-start.3 = (bf16[1280,512]{0,1:T(8,128)(2,1)}, bf16[1280,512]{0,1:T(8,128)(2,1)S(1)}, u32[]{:S(2)}) copy-start(bf16[1280,512]{0,1:T(8,128)(2,1)S(1)} %convolution_convert_fusion.6) | copy-start | bytes 3932164
  882.9 160.8 %copy-start.21 = (bf16[1280,8,32]{0,2,1:T(8,128)(2,1)S(1)}, bf16[1280,8,32]{0,2,1:T(8,128)(2,1)}, u32[]{:S(2)}) copy-start(bf16[1280,8,32]{0,2,1:T(8,128)(2,1)} %get-tuple-element.124) | copy-start | bytes 1966084
  882.9 160.8 %copy-start.22 = (bf16[1280,8,32]{0,2,1:T(8,128)(2,1)S(1)}, bf16[1280,8,32]{0,2,1:T(8,128)(2,1)}, u32[]{:S(2)}) copy-start(bf16[1280,8,32]{0,2,1:T(8,128)(2,1)} %get-tuple-element.125) | copy-start | bytes 1966084
  1081.1 128.4 %reduce-scatter.5.cloned.1.call-start = ((), (), s32[]{:S(2)}) async-start(), calls=%async_computation.9 | async-start | bytes 6553600 | tf_op jit(solution)/shard_map/reduce_scatter | solution.py:214
  1153.3 138.4 %all-reduce.19.cloned.1.call-start = ((), (), s32[]{:S(2)}) async-start(), calls=%async_computation.10 | async-start | bytes 5242880 | tf_op jit(solution)/shard_map/psum | solution.py:237
  1200.0 5.5 copy-start.32
  1200.1 5.4 copy-start.34
  1201.6 3.9 copy-start.68
  1205.5 4.0 copy-start.40
  1209.5 82.3 %copy-start.44 = (f32[1280]{0:T(1024)S(1)}, f32[1280]{0:T(1024)}, u32[]{:S(2)}) copy-start(f32[1280]{0:T(1024)} %copy-done.43) | copy-start | bytes 15364
  1209.5 82.3 %copy-start.50 = (f32[1024]{0:T(1024)S(1)}, f32[1024]{0:T(1024)}, u32[]{:S(2)}) copy-start(f32[1024]{0:T(1024)} %param.20) | copy-start | bytes 12292
  1217.0 141.9 %all-reduce.21.cloned.1.call-start = ((), (), s32[]{:S(2)}) async-start(), calls=%async_computation.11 | async-start | bytes 4194304 | tf_op jit(solution)/shard_map/psum | solution.py:13
  1291.7 5.0 copy-start.14
  1296.8 6.5 copy-start.63
  1307.3 9.0 copy-start.12
  1307.4 8.9 copy-start.46
  1307.4 8.9 copy-start.52
  1307.4 8.9 copy-start.57
  1307.4 141.0 %all-reduce.23.cloned.1.call-start = ((), (), s32[]{:S(2)}) async-start(), calls=%async_computation.12 | async-start | bytes 4194304 | tf_op jit(solution)/shard_map/psum | solution.py:14
  1307.4 8.9 copy-start.16
  1307.5 8.9 copy-start.74
  1358.9 338.7 %all-reduce.25.cloned.1.call-start = ((), (), s32[]{:S(2)}) async-start(), calls=%async_computation.13 | async-start | bytes 25690112 | tf_op jit(solution)/shard_map/psum | solution.py:254
  1359.1 8.9 copy-start.29
  1359.1 8.9 copy-start.69
  1368.0 2.6 copy-start.26
  1378.3 38.3 %copy-start.24 = (bf16[1280,1024,1]{1,0,2:T(8,128)(2,1)S(1)}, bf16[1280,1024,1]{1,0,2:T(8,128)(2,1)}, u32[]{:S(2)}) copy-start(bf16[1280,1024,1]{1,0,2:T(8,128)(2,1)} %copy-done.23) | copy-start | bytes 7864324
  1697.6 3.0 copy-start.39
  1697.6 4.6 copy-start.38
  1700.6 3.2 copy-start.37
  1702.3 3.2 copy-start.19
  1705.4 3.0 copy-start.18
  1708.4 3.0 copy-start.17
  1711.3 3.3 copy-start.1
  (23 other events, 37.8 us)
Sparse Core Ops, SparseCore 0:
  15.2 133.2 all-reduce.10
  160.5 40.4 all-gather.4
  235.0 40.4 all-gather.2
  446.2 74.6 all-reduce.12
  549.5 74.3 all-reduce.14
  652.2 74.3 all-reduce.16
  1081.2 51.3 reduce-scatter.2
  1153.5 51.3 reduce-scatter.4
  1217.1 74.5 all-reduce.18
  1307.5 51.3 all-reduce.20
  1361.3 87.0 all-reduce.22
  1455.8 241.7 all-reduce.24
